TPU v7x, 256 devices: a whole 4x4x8 slice. The times are simulated.
256 devices in a mesh: col: 16 (over x_lo, z), tile: 16 (over y, x_hi, core).
Axes of the slice: x: 4 (x_hi: 2, x_lo: 2; x = x_hi * 2 + x_lo), y: 4, z: 8, core: 2. Of those that a mesh axis runs over, the one named last changes fastest.
Arguments:
- initial_image: float32 [65536, 2048], P('tile', 'col'), may hold values from -6 to 6
- panels: float32 [16, 256, 65536], P('col', None, 'tile'), may hold values from -0.0234375 to 0.0234375
- sinogram: float32 [16, 256, 2048], P(None, 'tile', 'col'), may hold values from -6 to 6
- subset_order: int32 [3], replicated, may hold values from 0 to 15
- step_sizes: float32 [3], replicated, may hold values from 0.5 to 1
Outputs:
- final_image: float32 [65536, 2048], P('tile', 'col')
- final_duals: float32 [16, 256, 2048], P(None, 'tile', 'col')
Inputs may be any that keep to these rules, and one draw needn't show every extreme that they name: `subset_order`: repeats may occur.
All inputs are finite; a program needn't handle non-finite values.
Results may differ from a plain program's by a relative error of at most 0.00013.
Values sent between devices are 32-bit elements; how exact they have to be, the bound alone decides.
A program may use at most 128 MiB of HBM per device.

v0:
```python
import jax
import jax.numpy as jnp
from jax import lax
from jax.sharding import PartitionSpec as P

WIDTH = 512
ITERS = 3


penalty = 0.2
smoothing = 1.0


def shifted(value, axis, by):
    count = lax.axis_size(axis)
    pairs = [(i, i + by) for i in range(count) if 0 <= i + by < count]
    return lax.ppermute(value, axis, pairs)


def broadcast(value, axis, root):
    mine = lax.axis_index(axis) == root
    return lax.psum(jnp.where(mine, value, jnp.zeros_like(value)), axis)


def split_up(value, dim, count):
    lengths = value.shape
    tiles = value.reshape(*lengths[:dim], count, lengths[dim] // count, *lengths[dim + 1 :])
    return jnp.moveaxis(tiles, dim, 0)


def summed_on_arrival(value, axis, dim):
    count = lax.axis_size(axis)
    tiles = lax.all_to_all(split_up(value, dim, count), axis, 0, 0, tiled=True)
    return jnp.sum(tiles, axis=0)


def sent_to_all(value, axis):
    copies = jnp.broadcast_to(value, (lax.axis_size(axis), *value.shape))
    return lax.all_to_all(copies, axis, split_axis=0, concat_axis=0, tiled=True)


def in_order(tiles, dim):
    tiles = jnp.moveaxis(tiles, 0, dim)
    lengths = tiles.shape
    return tiles.reshape(*lengths[:dim], lengths[dim] * lengths[dim + 1], *lengths[dim + 2 :])


def collect(value, axis, dim):
    tiles = sent_to_all(value, axis)
    return in_order(tiles, dim)


def divergence(estimate, rows_local, tile_index, total_rows):
    channels = estimate.shape[1]
    image_field = estimate.reshape(rows_local, WIDTH, channels)
    row_below = shifted(image_field[0:1], "tile", -1)
    extended = jnp.concatenate([image_field, row_below], axis=0)
    downward = extended[1:] - extended[:-1]
    global_row = tile_index * rows_local + lax.broadcasted_iota(jnp.int32, (rows_local, 1, 1), 0)
    downward = jnp.where(global_row < total_rows - 1, downward, jnp.zeros_like(downward))
    column_zero = jnp.zeros((rows_local, 1, channels), estimate.dtype)
    across = jnp.concatenate([image_field[:, 1:] - image_field[:, :-1], column_zero], axis=1)
    magnitude = jnp.sqrt(across * across + downward * downward + smoothing * smoothing)
    flux_across = across / magnitude
    flux_down = downward / magnitude
    flux_above = shifted(flux_down[rows_local - 1 :], "tile", 1)
    shifted_across = jnp.concatenate([column_zero, flux_across[:, :-1]], axis=1)
    shifted_down = jnp.concatenate([flux_above, flux_down[:-1]], axis=0)
    divergence_field = flux_across - shifted_across + flux_down - shifted_down
    return divergence_field.reshape(estimate.shape)


def per_device(initial_image, panels, sinogram, subset_order, step_sizes):
    dual_step = step_sizes[0]
    primal_step = step_sizes[1]
    extrapolate = step_sizes[2]
    tile_count = lax.axis_size("tile")
    tile_index = lax.axis_index("tile")
    rows_local = initial_image.shape[0] // WIDTH
    total_rows = rows_local * tile_count
    stored = panels.shape[0]
    rays_local = panels.shape[1] // tile_count
    subset_count = sinogram.shape[0]

    def primal(estimate, extrapolated):
        field_div = divergence(estimate, rows_local, tile_index, total_rows)
        return estimate - primal_step * extrapolated + primal_step * penalty * field_div

    estimate = initial_image
    dual_state = jnp.zeros(sinogram.shape, jnp.float32)
    accumulated = jnp.zeros(initial_image.shape, jnp.float32)
    extrapolated = jnp.zeros(initial_image.shape, jnp.float32)
    for iteration in range(ITERS):
        estimate = primal(estimate, extrapolated)
        subset = subset_order[iteration]
        owner_index = subset // stored
        own_panel = lax.dynamic_index_in_dim(panels, subset % stored, 0, keepdims=False)
        operator_panel = broadcast(own_panel, "col", owner_index)
        current = lax.dynamic_index_in_dim(dual_state, subset, 0, keepdims=False)
        measured = lax.dynamic_index_in_dim(sinogram, subset, 0, keepdims=False)

        def partial_rows(first_row, row_count, operator_panel=operator_panel, estimate=estimate):
            return jnp.dot(
                operator_panel,
                estimate,
                precision=lax.Precision.HIGHEST,
                preferred_element_type=jnp.float32,
            )

        forward = summed_on_arrival(
            partial_rows(jnp.int32(0), rays_local * lax.axis_size("tile")), "tile", 0
        )
        updated = (current + dual_step * forward - dual_step * measured) / (1.0 + dual_step)
        change = updated - current

        def add_back(running, received, first_row, operator_panel=operator_panel):
            return lax.dot_general(
                operator_panel,
                received,
                (((0,), (0,)), ((), ())),
                precision=lax.Precision.HIGHEST,
                preferred_element_type=jnp.float32,
            )

        adjoint = add_back(
            jnp.zeros(estimate.shape, jnp.float32), collect(change, "tile", 0), jnp.int32(0)
        )
        dual_state = lax.dynamic_update_index_in_dim(dual_state, updated, subset, 0)
        accumulated = accumulated + adjoint
        extrapolated = accumulated + extrapolate * subset_count * adjoint
    final_image = primal(estimate, extrapolated)
    return (final_image, dual_state)


def solution(mesh):
    in_specs = (P("tile", "col"), P("col", None, "tile"), P(None, "tile", "col"), P(), P())
    out_specs = (P("tile", "col"), P(None, "tile", "col"))
    return jax.shard_map(
        per_device, mesh=mesh, in_specs=in_specs, out_specs=out_specs, check_vma=False
    )
```

profile of v0, /device:TPU:1, one launch (start us, length us, event | category | flops | bytes accessed | tf_op | source)
XLA Modules:
  0.0 470.2 jit_solution(4635605213795774346)
XLA Ops:
  7.2 1.4 fusion.37
  10.4 7.2 %select_bitcast_fusion = (f32[256,4096]{1,0:T(8,128)}, f32[256,4096]{1,0:T(8,128)}, f32[256,4096]{1,0:T(8,128)}) fusion(f32[1,256,4096]{2,1,0:T(8,128)} %param.6, pred[]{:T(512)S(6)} %eq.15, pred[]{:T(512)S(6)} %eq.13, pred[]{:T(512)S(6)} %eq.14), kind=kLoop, calls=%fused_computation | loop fusion | flops 3145728 | bytes 16777220 | tf_op jit(solution)/shard_map/jit(_where)/select_n | solution.py:22
  17.6 1.6 copy-done.4
  19.2 5.1 %collective-permute-start = (f32[1,512,128]{2,1,0:T(8,128)S(1)}, f32[1,512,128]{2,1,0:T(8,128)S(1)}, u32[]{:S(2)}, u32[]{:S(2)}) collective-permute-start(f32[1,512,128]{2,1,0:T(8,128)S(1)} %slice_bitcast_fusion.3), channel_id=1, source_target_pairs={{1,0},{2,1},{3,2},{4,3},{5,4},{6,5},{7,6},{8,7},{9,8},{10,9},{11,1... | collective-permute-start | bytes 786440 | tf_op jit(solution)/shard_map/ppermute | solution.py:17
  24.5 4.7 %collective-permute-done = f32[1,512,128]{2,1,0:T(8,128)S(1)} collective-permute-done((f32[1,512,128]{2,1,0:T(8,128)S(1)}, f32[1,512,128]{2,1,0:T(8,128)S(1)}, u32[]{:S(2)}, u32[]{:S(2)}) %collective-permute-start) | collective-permute-done | bytes 262176 | tf_op jit(solution)/shard_map/ppermute | solution.py:17
  29.2 2.5 fusion.22
  31.7 1.4 copy-done.6
  33.1 2.1 collective-permute-start.1
  38.7 0.7 fusion.36
  43.8 1.6 slice.156
  45.4 119.4 %collective-permute-done.1 = f32[1,512,128]{2,1,0:T(8,128)S(1)} collective-permute-done((f32[1,512,128]{2,1,0:T(8,128)S(1)}, f32[1,512,128]{2,1,0:T(8,128)S(1)}, u32[]{:S(2)}, u32[]{:S(2)}) %collective-permute-start.1) | collective-permute-done | bytes 262176 | tf_op jit(solution)/shard_map/ppermute | solution.py:17
  164.8 2.9 fusion.11
  167.7 0.2 bitcast_add_fusion.2
  168.0 1.9 collective-permute-start.2
  170.1 7.8 %collective-permute-done.2 = f32[1,512,128]{2,1,0:T(8,128)S(1)} collective-permute-done((f32[1,512,128]{2,1,0:T(8,128)S(1)}, f32[1,512,128]{2,1,0:T(8,128)S(1)}, u32[]{:S(2)}, u32[]{:S(2)}) %collective-permute-start.2) | collective-permute-done | bytes 262176 | tf_op jit(solution)/shard_map/ppermute | solution.py:17
  177.9 2.5 fusion.20
  180.4 1.5 slice.162
  181.9 0.4 copy-done.8
  182.3 1.9 collective-permute-start.3
  184.2 122.3 %all-reduce.11.cloned.1.call-done = (f32[256,4096]{1,0:T(8,128)}, f32[256,4096]{1,0:T(8,128)}, f32[256,4096]{1,0:T(8,128)}) async-done(((f32[256,4096]{1,0:T(8,128)}, f32[256,4096]{1,0:T(8,128)}, f32[256,4096]{1,0:T(8,128)}), (f32[256,4096]{1,0:T(8,128)}, f32[256,4096]{1,0:T(8,128)}, f32[256,4096]{1,0:T(8,128)})) %all-reduce.11.cloned.1.call-update) | async-done | bytes 12582928 | tf_op jit(solution)/shard_map/psum | solution.py:22
  306.5 5.9 %fusion.38 = f32[256,128]{1,0:T(8,128)} fusion(f32[256,4096]{1,0:T(8,128)} %get-tuple-element.2, f32[4096,128]{1,0:T(8,128)S(1)} %bitcast_add_fusion.2), kind=kOutput, calls=%fused_computation.77 | convolution fusion | flops 1610612736 | bytes 6422528 | tf_op jit(solution)/shard_map/dot_general | solution.py:103
  312.4 7.3 %all-to-all-start = ((f32[16,16,128]{2,1,0:T(8,128)}), f32[16,16,128]{2,1,0:T(8,128)S(1)}, u32[]{:S(2)}, u32[]{:S(2)}) async-start(f32[16,16,128]{2,1,0:T(8,128)} %bitcast.7), calls=%async_computation | async-start | bytes 262144 | tf_op jit(solution)/shard_map/all_to_all | solution.py:33
  319.7 5.1 %fusion.12 = f32[8,512,128]{2,1,0:T(8,128)} fusion(f32[7,512,128]{2,1,0:T(8,128)} %slice.162, f32[1,512,128]{2,1,0:T(8,128)S(1)} %collective-permute-done.3, f32[8,512,128]{2,1,0:T(8,128)} %copy-done.8, f32[8,512,128]{2,1,0:T(8,128)} %get-tuple-element.11, f32[8,511,128]{2,1,0:T(8,128)} %bitcast.111, f32[]{:T(128)S(6)} %mul.181), kind=kLoop, calls=%fused_computation.26 | loop fusion | flops 2621440 | bytes 10481668 | tf_op jit(solution)/shard_map/mul | solution.py:87
  324.9 2.5 all-to-all-done
  327.4 1.4 fusion.35
  328.8 0.7 broadcast_in_dim.35
  329.4 5.0 %all-to-all-start.1 = ((f32[16,16,128]{2,1,0:T(8,128)}), f32[16,16,128]{2,1,0:T(8,128)S(1)}, u32[]{:S(2)}, u32[]{:S(2)}) async-start(f32[16,16,128]{2,1,0:T(8,128)} %broadcast_in_dim.35), calls=%async_computation.1 | async-start | bytes 262144 | tf_op jit(solution)/shard_map/all_to_all | solution.py:39
  334.5 1.4 fusion.34
  335.9 6.1 %all-to-all-done.1 = f32[16,16,128]{2,1,0:T(8,128)S(1)} async-done(((f32[16,16,128]{2,1,0:T(8,128)}), f32[16,16,128]{2,1,0:T(8,128)S(1)}, u32[]{:S(2)}, u32[]{:S(2)}) %all-to-all-start.1) | async-done | bytes 131104 | tf_op jit(solution)/shard_map/all_to_all | solution.py:39
  342.0 11.8 %fusion.2 = (f32[4096,128]{1,0:T(8,128)S(1)}, f32[4096,128]{1,0:T(8,128)}) fusion(f32[4096,128]{1,0:T(8,128)S(1)} %bitcast_add_fusion.2, f32[8,512,128]{2,1,0:T(8,128)} %fusion.12, f32[]{:T(128)} %bitcast.10, f32[]{:T(128)} %bitcast, f32[256,4096]{1,0:T(8,128)} %get-tuple-element.2, f32[256,128]{1,0:T(8,128)S(1)} %bitcast.115), kind=kOutput, calls=%fused_computation.6 | convolution fusion | flops 1613234176 | bytes 12713992 | tf_op jit(solution)/shard_map/dot_general | solution.py:117
  353.8 4.1 fusion.39
  357.9 4.0 all-to-all-start.2
  361.9 2.1 collective-permute-start.4
  364.0 4.0 slice_subtract_fusion.1
  368.0 1.6 all-to-all-done.2
  369.6 1.5 collective-permute-done.4
  371.1 4.1 fusion.18
  375.1 1.4 copy-done.9
  376.5 1.9 collective-permute-start.5
  378.5 1.4 fusion.32
  379.9 0.7 broadcast_in_dim.37
  380.5 8.6 %all-to-all-start.3 = ((f32[16,16,128]{2,1,0:T(8,128)}), f32[16,16,128]{2,1,0:T(8,128)S(1)}, u32[]{:S(2)}, u32[]{:S(2)}) async-start(f32[16,16,128]{2,1,0:T(8,128)} %broadcast_in_dim.37), calls=%async_computation.3 | async-start | bytes 262144 | tf_op jit(solution)/shard_map/all_to_all | solution.py:39
  389.1 1.5 fusion.30
  390.7 1.6 slice.168
  392.3 4.1 fusion.13
  396.4 0.2 all-to-all-done.3
  396.6 12.7 %bitcast_add_fusion.1 = (f32[4096,128]{1,0:T(8,128)S(1)}, f32[4096,128]{1,0:T(8,128)}) fusion(f32[8,512,128]{2,1,0:T(8,128)} %fusion.13, f32[4096,128]{1,0:T(8,128)S(1)} %copy-done.1, f32[]{:T(128)} %bitcast.10, f32[]{:T(128)} %bitcast, f32[4096,128]{1,0:T(8,128)} %get-tuple-element.25, f32[256,4096]{1,0:T(8,128)} %get-tuple-element.3, ...), kind=kOutput, calls=%fused_computation.32 | convolution fusion | flops 1613758464 | bytes 14811144 | tf_op jit(solution)/shard_map/dot_general | solution.py:117
  409.4 4.1 fusion.40
  413.5 7.0 %all-to-all-start.4 = ((f32[16,16,128]{2,1,0:T(8,128)}), f32[16,16,128]{2,1,0:T(8,128)S(1)}, u32[]{:S(2)}, u32[]{:S(2)}) async-start(f32[16,16,128]{2,1,0:T(8,128)} %bitcast.28), calls=%async_computation.4 | async-start | bytes 262144 | tf_op jit(solution)/shard_map/all_to_all | solution.py:33
  420.5 4.0 slice_subtract_fusion
  424.5 2.0 collective-permute-start.6
  426.5 1.6 all-to-all-done.4
  428.2 1.4 fusion.27
  429.6 0.7 broadcast_in_dim.38
  430.2 6.2 %all-to-all-start.5 = ((f32[16,16,128]{2,1,0:T(8,128)}), f32[16,16,128]{2,1,0:T(8,128)S(1)}, u32[]{:S(2)}, u32[]{:S(2)}) async-start(f32[16,16,128]{2,1,0:T(8,128)} %broadcast_in_dim.38), calls=%async_computation.5 | async-start | bytes 262144 | tf_op jit(solution)/shard_map/all_to_all | solution.py:39
  436.4 1.4 fusion.25
  437.8 4.1 fusion.16
  441.9 1.4 copy-done.11
  443.3 5.0 %collective-permute-start.7 = (f32[1,512,128]{2,1,0:T(8,128)S(1)}, f32[1,512,128]{2,1,0:T(8,128)S(1)}, u32[]{:S(2)}, u32[]{:S(2)}) collective-permute-start(f32[1,512,128]{2,1,0:T(8,128)S(1)} %slice.173), channel_id=1, source_target_pairs={{0,1},{1,2},{2,3},{3,4},{4,5},{5,6},{6,7},{7,8},{8,9},{9,10},{10,1... | collective-permute-start | bytes 786440 | tf_op jit(solution)/shard_map/ppermute | solution.py:17
  448.4 8.8 %fusion.41 = f32[4096,128]{1,0:T(8,128)S(1)} fusion(f32[256,4096]{1,0:T(8,128)} %get-tuple-element.4, f32[256,128]{1,0:T(8,128)S(1)} %bitcast.116), kind=kOutput, calls=%fused_computation.80 | convolution fusion | flops 1610612736 | bytes 6422528 | tf_op jit(solution)/shard_map/dot_general | solution.py:117
  457.4 1.4 copy-done.13
  458.8 0.5 fusion.14
  459.3 1.1 copy-done.16
  460.4 2.5 bitcast_add_fusion
  (54 shorter events, 0.9 us)
Async XLA Ops:
  7.2 299.4 %all-reduce.11.cloned.1.call-start = ((), (), s32[]{:S(2)}) async-start(), calls=%async_computation.6 | async-start | bytes 25165824 | tf_op jit(solution)/shard_map/psum | solution.py:22
  17.6 1.6 copy-start.4
  19.2 10.1 %collective-permute-start = (f32[1,512,128]{2,1,0:T(8,128)S(1)}, f32[1,512,128]{2,1,0:T(8,128)S(1)}, u32[]{:S(2)}, u32[]{:S(2)}) collective-permute-start(f32[1,512,128]{2,1,0:T(8,128)S(1)} %slice_bitcast_fusion.3), channel_id=1, source_target_pairs={{1,0},{2,1},{3,2},{4,3},{5,4},{6,5},{7,6},{8,7},{9,8},{10,9},{11,1... | collective-permute-start | bytes 786440 | tf_op jit(solution)/shard_map/ppermute | solution.py:17
  24.5 14.2 %copy-start.18 = (f32[3]{0:T(128)S(1)}, f32[3]{0:T(128)}, u32[]{:S(2)}) copy-start(f32[3]{0:T(128)} %param.9) | copy-start | bytes 40
  31.7 1.4 copy-start.6
  33.1 131.7 %copy-start.7 = (f32[8,512,128]{2,1,0:T(8,128)S(1)}, f32[8,512,128]{2,1,0:T(8,128)}, u32[]{:S(2)}) copy-start(f32[8,512,128]{2,1,0:T(8,128)} %copy-done.6) | copy-start | bytes 6291460
  33.1 131.7 %collective-permute-start.1 = (f32[1,512,128]{2,1,0:T(8,128)S(1)}, f32[1,512,128]{2,1,0:T(8,128)S(1)}, u32[]{:S(2)}, u32[]{:S(2)}) collective-permute-start(f32[1,512,128]{2,1,0:T(8,128)S(1)} %slice.155), channel_id=1, source_target_pairs={{0,1},{1,2},{2,3},{3,4},{4,5},{5,6},{6,7},{7,8},{8,9},{9,10},{10,1... | collective-permute-start | bytes 786440 | tf_op jit(solution)/shard_map/ppermute | solution.py:17
  164.8 2.9 copy-start.5
  168.0 9.9 %collective-permute-start.2 = (f32[1,512,128]{2,1,0:T(8,128)S(1)}, f32[1,512,128]{2,1,0:T(8,128)S(1)}, u32[]{:S(2)}, u32[]{:S(2)}) collective-permute-start(f32[1,512,128]{2,1,0:T(8,128)S(1)} %slice_bitcast_fusion.2), channel_id=1, source_target_pairs={{1,0},{2,1},{3,2},{4,3},{5,4},{6,5},{7,6},{8,7},{9,8},{10,9},{11,1... | collective-permute-start | bytes 786440 | tf_op jit(solution)/shard_map/ppermute | solution.py:17
  180.4 1.9 copy-start.8
  182.3 137.4 %collective-permute-start.3 = (f32[1,512,128]{2,1,0:T(8,128)S(1)}, f32[1,512,128]{2,1,0:T(8,128)S(1)}, u32[]{:S(2)}, u32[]{:S(2)}) collective-permute-start(f32[1,512,128]{2,1,0:T(8,128)S(1)} %slice.161), channel_id=1, source_target_pairs={{0,1},{1,2},{2,3},{3,4},{4,5},{5,6},{6,7},{7,8},{8,9},{9,10},{10,1... | collective-permute-start | bytes 786440 | tf_op jit(solution)/shard_map/ppermute | solution.py:17
  312.4 14.9 %all-to-all-start = ((f32[16,16,128]{2,1,0:T(8,128)}), f32[16,16,128]{2,1,0:T(8,128)S(1)}, u32[]{:S(2)}, u32[]{:S(2)}) async-start(f32[16,16,128]{2,1,0:T(8,128)} %bitcast.7), calls=%async_computation | async-start | bytes 262144 | tf_op jit(solution)/shard_map/all_to_all | solution.py:33
  329.4 12.5 %all-to-all-start.1 = ((f32[16,16,128]{2,1,0:T(8,128)}), f32[16,16,128]{2,1,0:T(8,128)S(1)}, u32[]{:S(2)}, u32[]{:S(2)}) async-start(f32[16,16,128]{2,1,0:T(8,128)} %broadcast_in_dim.35), calls=%async_computation.1 | async-start | bytes 262144 | tf_op jit(solution)/shard_map/all_to_all | solution.py:39
  342.0 11.8 %copy-start.15 = (f32[256,4096]{1,0:T(8,128)S(1)}, f32[256,4096]{1,0:T(8,128)}, u32[]{:S(2)}) copy-start(f32[256,4096]{1,0:T(8,128)} %get-tuple-element.3) | copy-start | bytes 12582916
  353.8 4.2 copy-start
  357.9 11.7 %all-to-all-start.2 = ((f32[16,16,128]{2,1,0:T(8,128)}), f32[16,16,128]{2,1,0:T(8,128)S(1)}, u32[]{:S(2)}, u32[]{:S(2)}) async-start(f32[16,16,128]{2,1,0:T(8,128)} %bitcast.18), calls=%async_computation.2 | async-start | bytes 262144 | tf_op jit(solution)/shard_map/all_to_all | solution.py:33
  361.9 9.2 %collective-permute-start.4 = (f32[1,512,128]{2,1,0:T(8,128)S(1)}, f32[1,512,128]{2,1,0:T(8,128)S(1)}, u32[]{:S(2)}, u32[]{:S(2)}) collective-permute-start(f32[1,512,128]{2,1,0:T(8,128)S(1)} %slice_bitcast_fusion.1), channel_id=1, source_target_pairs={{1,0},{2,1},{3,2},{4,3},{5,4},{6,5},{7,6},{8,7},{9,8},{10,9},{11,1... | collective-permute-start | bytes 786440 | tf_op jit(solution)/shard_map/ppermute | solution.py:17
  364.0 7.0 %copy-start.1 = (f32[4096,128]{1,0:T(8,128)S(1)}, f32[4096,128]{1,0:T(8,128)}, u32[]{:S(2)}) copy-start(f32[4096,128]{1,0:T(8,128)} %copy-done) | copy-start | bytes 6291460
  375.1 1.4 copy-start.9
  376.5 15.8 %collective-permute-start.5 = (f32[1,512,128]{2,1,0:T(8,128)S(1)}, f32[1,512,128]{2,1,0:T(8,128)S(1)}, u32[]{:S(2)}, u32[]{:S(2)}) collective-permute-start(f32[1,512,128]{2,1,0:T(8,128)S(1)} %slice.167), channel_id=1, source_target_pairs={{0,1},{1,2},{2,3},{3,4},{4,5},{5,6},{6,7},{7,8},{8,9},{9,10},{10,1... | collective-permute-start | bytes 786440 | tf_op jit(solution)/shard_map/ppermute | solution.py:17
  380.5 16.1 %all-to-all-start.3 = ((f32[16,16,128]{2,1,0:T(8,128)}), f32[16,16,128]{2,1,0:T(8,128)S(1)}, u32[]{:S(2)}, u32[]{:S(2)}) async-start(f32[16,16,128]{2,1,0:T(8,128)} %broadcast_in_dim.37), calls=%async_computation.3 | async-start | bytes 262144 | tf_op jit(solution)/shard_map/all_to_all | solution.py:39
  389.1 3.2 copy-start.10
  396.6 12.7 %copy-start.14 = (f32[256,4096]{1,0:T(8,128)S(1)}, f32[256,4096]{1,0:T(8,128)}, u32[]{:S(2)}) copy-start(f32[256,4096]{1,0:T(8,128)} %get-tuple-element.4) | copy-start | bytes 12582916
  409.4 4.1 copy-start.2
  413.5 14.6 %all-to-all-start.4 = ((f32[16,16,128]{2,1,0:T(8,128)}), f32[16,16,128]{2,1,0:T(8,128)S(1)}, u32[]{:S(2)}, u32[]{:S(2)}) async-start(f32[16,16,128]{2,1,0:T(8,128)} %bitcast.28), calls=%async_computation.4 | async-start | bytes 262144 | tf_op jit(solution)/shard_map/all_to_all | solution.py:33
  420.5 4.0 copy-start.3
  424.5 13.3 %collective-permute-start.6 = (f32[1,512,128]{2,1,0:T(8,128)S(1)}, f32[1,512,128]{2,1,0:T(8,128)S(1)}, u32[]{:S(2)}, u32[]{:S(2)}) collective-permute-start(f32[1,512,128]{2,1,0:T(8,128)S(1)} %slice_bitcast_fusion), channel_id=1, source_target_pairs={{1,0},{2,1},{3,2},{4,3},{5,4},{6,5},{7,6},{8,7},{9,8},{10,9},{11,1... | collective-permute-start | bytes 786440 | tf_op jit(solution)/shard_map/ppermute | solution.py:17
  430.2 18.1 %all-to-all-start.5 = ((f32[16,16,128]{2,1,0:T(8,128)}), f32[16,16,128]{2,1,0:T(8,128)S(1)}, u32[]{:S(2)}, u32[]{:S(2)}) async-start(f32[16,16,128]{2,1,0:T(8,128)} %broadcast_in_dim.38), calls=%async_computation.5 | async-start | bytes 262144 | tf_op jit(solution)/shard_map/all_to_all | solution.py:39
  437.8 4.1 copy-start.17
  441.9 1.4 copy-start.11
  443.3 14.1 %collective-permute-start.7 = (f32[1,512,128]{2,1,0:T(8,128)S(1)}, f32[1,512,128]{2,1,0:T(8,128)S(1)}, u32[]{:S(2)}, u32[]{:S(2)}) collective-permute-start(f32[1,512,128]{2,1,0:T(8,128)S(1)} %slice.173), channel_id=1, source_target_pairs={{0,1},{1,2},{2,3},{3,4},{4,5},{5,6},{6,7},{7,8},{8,9},{9,10},{10,1... | collective-permute-start | bytes 786440 | tf_op jit(solution)/shard_map/ppermute | solution.py:17
  448.4 8.8 %copy-start.12 = (f32[8,512,128]{2,1,0:T(8,128)S(1)}, f32[8,512,128]{2,1,0:T(8,128)}, u32[]{:S(2)}) copy-start(f32[8,512,128]{2,1,0:T(8,128)} %copy-done.11) | copy-start | bytes 6291460
  457.2 1.6 copy-start.13
  458.8 1.6 copy-start.16
Sparse Core Ops, SparseCore 0:
  17.7 288.7 all-reduce.10
where the time goes:
time: 478 us; the launch traced here: 470 us
  waiting for transfers between devices  268 us (56%)
  starting transfers between devices  60.2 us (13%)
  other arithmetic  52.6 us (11%)
  matrix products  47.5 us (10%)
  between operations  24.5 us (5%)
  local copies, waits for them, and re-layouts  17.8 us (4%)
    ppermute x8, waiting for transfers between devices, shifted(): return lax.ppermute(value, axis, pairs)  133 us
    psum x1, waiting for transfers between devices, broadcast(): return lax.psum(jnp.where(mine, value, jnp.zeros_like(value)), axis)  122 us
    dot_general x3, matrix products, add_back(): lax.dot_general(operator_panel, received, (((0,), (0,)), ((), ())), preci...  33.4 us
    ppermute x8, starting transfers between devices, shifted(): return lax.ppermute(value, axis, pairs)  22.1 us
    all_to_all x3, starting transfers between devices, sent_to_all(): return lax.all_to_all(copies, axis, split_axis=0, concat_axis=0, tiled=True)  19.8 us
    all_to_all x3, starting transfers between devices, summed_on_arrival(): tiles = lax.all_to_all(split_up(value, dim, count), axis, 0, 0, tiled=True)  18.3 us
    dot_general x3, matrix products, partial_rows(): jnp.dot(operator_panel, estimate, precision=lax.Precision.HIGHEST, prefer...  14.1 us
    div x4, other arithmetic, divergence(): flux_across = across / magnitude  13.2 us
  transfers between devices with their start and end apart: 15, of which 10 were waited for; matrix products, arithmetic and copies ran while one was open for 12% of the time, Pallas kernels for 0%

commit v1 on v0

v1 whole, which is shorter than its diff:
```python
import jax
import jax.numpy as jnp
from jax import lax
from jax.experimental import pallas as pl
from jax.experimental.pallas import tpu as pltpu
from jax.sharding import PartitionSpec as P

MESH = pl.DeviceIdType.MESH
WIDTH = 512
ITERS = 3
PENALTY = 0.2
RING = 8
LAG = 3
COUNTS = (11, 11, 10)
CHUNK = 4
CHUNKS = 88
STEPS = CHUNKS + 8 * LAG
SLOTS = 8
F32 = jnp.float32
BF16 = jnp.bfloat16
PLUS, MINUS, ACROSS, OWN = 0, 1, 2, 3


def halves(x):
    high = x.astype(BF16)
    return high, (x - high.astype(F32)).astype(BF16)


def matmul(a, b, dims):
    return lax.dot_general(a, b, (dims, ((), ())), preferred_element_type=F32)


def kernel(base, steps, image, panel, measured, turns, again, out, duals,
           recv, staging, u, w, acc, high, low, above, below, flux,
           fwd, shares, change_own, changes,
           recv_sem, send_sem, own_sem, halo_send, halo_recv, sum_send, sum_recv, all_send, all_recv):
    col, tile = lax.axis_index("col"), lax.axis_index("tile")
    tiles = lax.axis_size("tile")
    rail, z = col // RING, lax.rem(col, RING)
    up = rail * RING + lax.rem(z + 1, RING)
    down = rail * RING + lax.rem(z + RING - 1, RING)
    partner = (1 - rail) * RING + z
    next_tile, prev_tile = lax.rem(tile + 1, tiles), lax.rem(tile + tiles - 1, tiles)
    links = ((PLUS, up), (MINUS, down), (ACROSS, partner))

    blocks = panel.shape[3] // 128
    def own_copy(tree, block):
        count = COUNTS[tree]
        return pltpu.make_async_copy(
            panel.at[0, pl.ds(sum(COUNTS[:tree]), count), :,
                     pl.ds(pl.multiple_of(block * 128, 128), 128)],
            recv.at[OWN, tree, pl.ds(block * count, count)],
            own_sem.at[tree, block],
        )

    for tree in range(3):
        @pl.loop(0, blocks)
        def _(block, tree=tree):
            own_copy(tree, block).start()

    barrier = pltpu.get_barrier_semaphore()
    for _, where in links:
        pl.semaphore_signal(barrier, inc=1, device_id={"col": where}, device_id_type=MESH)
    for d in range(1, tiles):
        pl.semaphore_signal(
            barrier, inc=1, device_id={"tile": lax.rem(tile + d, tiles)}, device_id_type=MESH)
    pl.semaphore_wait(barrier, tiles + 2)

    def halo_copies(source, m):
        last = source.shape[0] - WIDTH
        return (
            pltpu.make_async_remote_copy(
                source.at[pl.ds(0, WIDTH)], below.at[m], halo_send.at[m, 0], halo_recv.at[m, 0],
                device_id={"tile": prev_tile}, device_id_type=MESH),
            pltpu.make_async_remote_copy(
                source.at[pl.ds(last, WIDTH)], above.at[m], halo_send.at[m, 1], halo_recv.at[m, 1],
                device_id={"tile": next_tile}, device_id_type=MESH),
        )

    for copy in halo_copies(image, 0):
        copy.start()

    for tree in range(3):
        @pl.loop(0, blocks)
        def _(block, tree=tree):
            own_copy(tree, block).wait()

    def hop(link, where, step, slot):
        return pltpu.make_async_remote_copy(
            staging.at[slot, link],
            recv.at[link, :, pl.ds(step * CHUNK, CHUNK)],
            send_sem.at[slot, link], recv_sem.at[slot, link],
            device_id={"col": where}, device_id_type=MESH)

    def arrival(link, step, slot):
        ref = recv.at[link, :, pl.ds(step * CHUNK, CHUNK)]
        return pltpu.make_async_copy(ref, ref, recv_sem.at[slot, link])

    def chunk(link, k, step):
        return recv[link, k, pl.ds(step * CHUNK, CHUNK)]

    for step in range(LAG):
        for tree, (link, where) in enumerate(links):
            for k in range(ITERS):
                staging[step, link, k] = chunk(OWN, tree, step)
        for link, where in links:
            hop(link, where, step, step).start()

    @pl.loop(LAG, STEPS)
    def _(step):
        slot = lax.rem(step, SLOTS)
        came = step - LAG
        for link, _ in links:
            arrival(link, came, lax.rem(came, SLOTS)).wait()

        @pl.when(step >= SLOTS)
        def _():
            for link, where in links:
                hop(link, where, step - SLOTS, slot).wait_send()

        mine = jnp.minimum(step, CHUNKS - 1)
        for k in range(ITERS):
            plus, minus, across = (chunk(link, k, came) for link in (PLUS, MINUS, ACROSS))
            root, first_turn, second_turn, near = (turns[k, n] == 1 for n in range(4))
            staging[slot, PLUS, k] = jnp.where(
                root, chunk(OWN, 0, mine), jnp.where(first_turn, across, plus))
            staging[slot, MINUS, k] = jnp.where(
                root, chunk(OWN, 1, mine), jnp.where(second_turn, across, minus))
            staging[slot, ACROSS, k] = jnp.where(
                root, chunk(OWN, 2, mine), jnp.where(near, plus, minus))
        for link, where in links:
            hop(link, where, step, slot).start()

    for step in range(STEPS - LAG, STEPS):
        for link, _ in links:
            arrival(link, step, step % SLOTS).wait()
    for step in range(STEPS - SLOTS, STEPS):
        for link, where in links:
            hop(link, where, step, step % SLOTS).wait_send()

    dual_step, primal_step, extrapolate = steps[0], steps[1], steps[2]
    rows_local = u.shape[1] // WIDTH
    column = lax.broadcasted_iota(jnp.int32, (WIDTH, 128), 0)
    inner = column < WIDTH - 1
    top = jnp.full((WIDTH, 128), tile) == 0
    bottom = jnp.full((WIDTH, 128), tile) == tiles - 1

    def fluxes(row, under, cut):
        across = jnp.where(inner, pltpu.roll(row, WIDTH - 1, 0) - row, 0.0)
        drop = under - row
        if cut is not None:
            drop = jnp.where(cut, 0.0, drop)
        inverse = 1.0 / jnp.sqrt(across * across + drop * drop + 1.0)
        return across * inverse, drop * inverse

    def smooth(source, m, target):
        for copy in halo_copies(source, m):
            copy.wait()
        flux[...] = jnp.where(top, 0.0, fluxes(above[m], source[pl.ds(0, WIDTH), :], None)[1])

        def one(start, under, cut):
            row = source[pl.ds(start, WIDTH), :]
            right, drop = fluxes(row, under, cut)
            div = right - pltpu.roll(right, 1, 0) + drop - flux[...]
            flux[...] = drop
            target[pl.ds(start, WIDTH), :] = row + primal_step * PENALTY * div

        @pl.loop(0, rows_local - 1)
        def _(r):
            start = pl.multiple_of(r * WIDTH, WIDTH)
            one(start, source[pl.ds(pl.multiple_of(start + WIDTH, WIDTH), WIDTH), :], None)

        one((rows_local - 1) * WIDTH, below[m], bottom)

    smooth(image, 0, u.at[0])

    pairs = blocks // 2
    for k in range(ITERS):
        now = u.at[k]
        for copy in halo_copies(now, k + 1):
            copy.start()
        fwd[k] = jnp.zeros((256, 128), F32)

        @pl.loop(0, pairs)
        def _(q, now=now, k=k):
            def part(b):
                return jnp.concatenate([
                    recv[base[k, tree, 0], base[k, tree, 1], base[k, tree, 2] + (b * COUNTS[tree] + n)]
                    for tree in range(3) for n in range(COUNTS[tree])], axis=0)

            block = jnp.concatenate([part(2 * q), part(2 * q + 1)], axis=1)
            p_high, p_low = halves(block)
            high[q] = p_high
            low[q] = p_low
            x_high, x_low = halves(now[pl.ds(pl.multiple_of(q * 256, 256), 256), :])
            both = matmul(p_high, jnp.concatenate([x_high, x_low], axis=1), ((1,), (0,)))
            rest = matmul(p_low, x_high, ((1,), (0,)))
            fwd[k] += both[:, :128] + (both[:, 128:] + rest)

        def share(d, k=k):
            to = lax.rem(tile + d, tiles)
            return pltpu.make_async_remote_copy(
                fwd.at[k, pl.ds(pl.multiple_of(to * 16, 16), 16)], shares.at[k, d - 1],
                sum_send.at[k, d - 1], sum_recv.at[k, d - 1],
                device_id={"tile": to}, device_id_type=MESH)

        for d in range(1, tiles):
            share(d).start()

        smooth(now, k + 1, w)

        total = fwd[k, pl.ds(pl.multiple_of(tile * 16, 16), 16), :]
        for d in range(1, tiles):
            share(d).wait()
            total = total + shares[k, d - 1]
        current = jnp.zeros((16, 128), F32)
        for j in range(k):
            current = jnp.where(again[k, j] == 1, duals[j], current)
        updated = (current + dual_step * total - dual_step * measured[k]) / (1.0 + dual_step)
        duals[k] = updated
        change_own[k] = updated - current

        def spread(d, k=k):
            return pltpu.make_async_remote_copy(
                change_own.at[k], changes.at[k, d - 1],
                all_send.at[k, d - 1], all_recv.at[k, d - 1],
                device_id={"tile": lax.rem(tile + d, tiles)}, device_id_type=MESH)

        for d in range(1, tiles):
            spread(d).start()
        for d in range(1, tiles):
            spread(d).wait()
        fwd[k, pl.ds(pl.multiple_of(tile * 16, 16), 16), :] = change_own[k]
        for d in range(1, tiles):
            came = lax.rem(tile + tiles - d, tiles)
            fwd[k, pl.ds(pl.multiple_of(came * 16, 16), 16), :] = changes[k, d - 1]
        c_high, c_low = halves(fwd[k])
        c_both = jnp.concatenate([c_high, c_low], axis=1)

        @pl.loop(0, pairs)
        def _(q, k=k, c_high=c_high, c_both=c_both):
            both = matmul(high[q], c_both, ((0,), (0,)))
            rest = matmul(low[q], c_high, ((0,), (0,)))
            adjoint = both[:, :128] + (both[:, 128:] + rest)
            at = pl.ds(pl.multiple_of(q * 256, 256), 256)
            gathered = adjoint if k == 0 else acc[at, :] + adjoint
            if k < ITERS - 1:
                acc[at, :] = gathered
            pushed = gathered + extrapolate * 16.0 * adjoint
            result = w[at, :] - primal_step * pushed
            if k < ITERS - 1:
                u[k + 1, at, :] = result
            else:
                out[at, :] = result


def routes(order):
    col = lax.axis_index("col")
    rail, z = col // RING, col % RING
    i, same = (z - order % RING) % RING, rail == order // RING
    root = same & (i == 0)
    flags = jnp.stack([
        root,
        ~same & ((i == 0) | (i == 4)),
        ~same & ((i == 0) | (i == 5)),
        i <= 4,
    ], axis=1)
    turns = jnp.broadcast_to(
        flags.astype(jnp.int32)[:, :, None, None, None], (ITERS, 4, CHUNK, 8, 128))
    link = jnp.stack([
        jnp.where(same | (i == 0) | (i > 4), PLUS, ACROSS),
        jnp.where(same | (i <= 4), MINUS, ACROSS),
        jnp.where(same | (i == 0), ACROSS, jnp.where(i <= 4, PLUS, MINUS)),
    ], axis=1)
    depth = jnp.stack([
        jnp.where(same, i, jnp.where(i == 0, 9, i + 1)),
        jnp.where(same, 8 - i, 9 - i),
        jnp.where(same, jnp.where(i <= 4, i + 2, 10 - i), jnp.where(i <= 4, i + 1, 9 - i)),
    ], axis=1)
    k, tree = jnp.arange(ITERS)[:, None], jnp.arange(3)[None, :]
    mine = root[:, None]
    base = jnp.stack([
        jnp.where(mine, OWN, link),
        jnp.where(mine, tree, k),
        jnp.where(mine, 0, (depth - 1) * (LAG * CHUNK)),
    ], axis=2)
    again = jnp.broadcast_to(
        (order[:, None] == order[None, :]).astype(jnp.int32)[:, :, None, None],
        (ITERS, ITERS, 16, 128))
    return base.astype(jnp.int32), turns, again


def per_device(initial_image, panels, sinogram, subset_order, step_sizes):
    pixels, channels = initial_image.shape
    rays = sinogram.shape[1]
    tiles = lax.axis_size("tile")
    measured = jnp.stack([
        lax.dynamic_index_in_dim(sinogram, subset_order[k], 0, keepdims=False)
        for k in range(ITERS)])
    base, turns, again = routes(subset_order)
    tiled = panels.reshape(panels.shape[0], panels.shape[1] // 8, 8, panels.shape[2])
    vmem = pl.BlockSpec(memory_space=pltpu.VMEM)
    smem = pl.BlockSpec(memory_space=pltpu.SMEM)
    dma = pltpu.SemaphoreType.DMA
    blocks = panels.shape[2] // 128
    image, updates = pl.pallas_call(
        kernel,
        out_shape=(jax.ShapeDtypeStruct((pixels, channels), F32),
                   jax.ShapeDtypeStruct((ITERS, rays, channels), F32)),
        in_specs=[smem, smem, vmem, pl.BlockSpec(memory_space=pl.ANY), vmem, vmem, vmem],
        out_specs=(vmem, vmem),
        scratch_shapes=[
            pltpu.VMEM((4, ITERS, STEPS * CHUNK, 8, 128), F32),
            pltpu.VMEM((SLOTS, 3, ITERS, CHUNK, 8, 128), F32),
            pltpu.VMEM((ITERS, pixels, channels), F32),
            pltpu.VMEM((pixels, channels), F32),
            pltpu.VMEM((pixels, channels), F32),
            pltpu.VMEM((blocks // 2, 256, 256), BF16),
            pltpu.VMEM((blocks // 2, 256, 256), BF16),
            pltpu.VMEM((ITERS + 1, WIDTH, channels), F32),
            pltpu.VMEM((ITERS + 1, WIDTH, channels), F32),
            pltpu.VMEM((WIDTH, channels), F32),
            pltpu.VMEM((ITERS, rays * tiles, channels), F32),
            pltpu.VMEM((ITERS, tiles - 1, rays, channels), F32),
            pltpu.VMEM((ITERS, rays, channels), F32),
            pltpu.VMEM((ITERS, tiles - 1, rays, channels), F32),
            dma((SLOTS, 3)), dma((SLOTS, 3)), dma((3, blocks)),
            dma((ITERS + 1, 2)), dma((ITERS + 1, 2)),
            dma((ITERS, tiles - 1)), dma((ITERS, tiles - 1)),
            dma((ITERS, tiles - 1)), dma((ITERS, tiles - 1)),
        ],
        compiler_params=pltpu.CompilerParams(
            collective_id=0, has_side_effects=True, vmem_limit_bytes=62 * 1024 * 1024),
    )(base, step_sizes, initial_image, tiled, measured, turns, again)
    duals = jnp.zeros(sinogram.shape, F32)
    for k in range(ITERS):
        duals = lax.dynamic_update_index_in_dim(duals, updates[k], subset_order[k], 0)
    return image, duals


def solution(mesh):
    in_specs = (P("tile", "col"), P("col", None, "tile"), P(None, "tile", "col"), P(), P())
    out_specs = (P("tile", "col"), P(None, "tile", "col"))
    return jax.shard_map(
        per_device, mesh=mesh, in_specs=in_specs, out_specs=out_specs, check_vma=False
    )
```

time: 478 us -> 254 us (0.53); the launches traced: 470 us -> 253 us
  waiting for transfers between devices: 268 us -> 0 us
  Pallas kernels: 0 us -> 235 us
  starting transfers between devices: 60.2 us -> 0 us
  other arithmetic: 52.6 us -> 2.86 us
  matrix products: 47.5 us -> 0 us
  between operations: 24.5 us -> 6.25 us
  local copies, waits for them, and re-layouts: 17.8 us -> 9.45 us
    pallas_call x0 -> x1, Pallas kernels: none -> 235 us  [per_device(): pl.pallas_call(kernel, out_shape=(jax.ShapeDtypeStruct((pixels, channels)...]
    ppermute x8 -> x0, waiting for transfers between devices: 133 us -> none  [shifted(): return lax.ppermute(value, axis, pairs)]
    psum x1 -> x0, waiting for transfers between devices: 122 us -> none  [broadcast(): return lax.psum(jnp.where(mine, value, jnp.zeros_like(value)), axis)]
    dot_general x6 -> x0, matrix products: 47.5 us -> none  [the longest x3 33.4 us: add_back(): lax.dot_general(operator_panel, received, (((0,), (0,)), ((), ())), preci...]
    all_to_all x6 -> x0, starting transfers between devices: 38.1 us -> none  [the longest x3 19.8 us: sent_to_all(): return lax.all_to_all(copies, axis, split_axis=0, concat_axis=0, tiled=True)]
    ppermute x8 -> x0, starting transfers between devices: 22.1 us -> none  [shifted(): return lax.ppermute(value, axis, pairs)]
    div x5 -> x0, other arithmetic: 14.6 us -> none  [the longest x4 13.2 us: divergence(): flux_across = across / magnitude]
    mul x4 -> x0, other arithmetic: 12.6 us -> none  [primal(): primal_step * penalty * field_div]
  transfers between devices with their start and end apart: 15 -> 0, of which waited for: 10 -> 0; matrix products, arithmetic and copies ran while one was open for 12% -> 0% of each run, Pallas kernels for 0% -> 0%
where the time goes in v1:
time: 254 us; the launch traced here: 253 us
  Pallas kernels  235 us (93%)
  local copies, waits for them, and re-layouts  9.45 us (4%)
  between operations  6.25 us (2%)
  other arithmetic  2.86 us (1%)
    pallas_call x1, Pallas kernels, per_device(): pl.pallas_call(kernel, out_shape=(jax.ShapeDtypeStruct((pixels, channels)...  235 us

profile of v1, /device:TPU:1, one launch (start us, length us, event | category | flops | bytes accessed | tf_op | source)
XLA Modules:
  0.0 253.3 jit_solution(1474142281113348993)
XLA Ops:
  0.7 0.7 and_bitcast_fusion.1
  1.3 0.1 copy.25
  1.4 0.1 copy.24
  1.5 0.1 copy.23
  1.6 0.1 copy.28
  1.7 0.1 copy.27
  1.8 0.1 copy.26
  1.9 0.1 add_select_fusion
  2.0 0.7 pad_add_fusion.base
  2.7 1.3 fusion.11
  9.6 0.8 constant_dynamic-slice_fusion.2
  10.4 0.6 pad_maximum_fusion.measured
  11.0 0.1 copy.29
  11.1 0.8 broadcast_in_dim.91.turns
  11.8 0.8 compare_convert_fusion
  12.6 0.7 broadcast_in_dim.92.again
  13.3 234.7 %shard_map.68 = (f32[4096,128]{1,0:T(8,128)}, f32[3,16,128]{2,1,0:T(8,128)}) custom-call(s32[3,3,3]{2,1,0:T(4,128)} %pad_add_fusion.base, f32[3]{0:T(128)} %steps.1, f32[4096,128]{1,0:T(8,128)} %image.1, f32[1,32,8,4096]{3,2,1,0:T(8,128)} %bitcast.23, f32[3,16,128]{2,1,0:T(8,128)} %pad_maximum_fusion.measured, s32[3,4,4,8,128]{4,3,2,1,0:T(8,128)} %broadcast_in_dim.91.turns, ...), custom_call_target="tpu_custom_call" | custom-call | tf_op jit(solution)/shard_map/pallas_call | solution.py:306
  248.1 0.7 slice_dynamic-update-slice_fusion.2
  248.8 0.7 slice_dynamic-update-slice_fusion.1
  249.5 0.7 slice_dynamic-update-slice_fusion
  250.2 0.0 copy-start
  250.2 3.1 %copy.34 = f32[4096,128]{1,0:T(8,128)} copy(f32[4096,128]{1,0:T(8,128)} %get-tuple-element.29) | data formatting | bytes 4194304
  253.3 0.0 copy-done
  (4 shorter events, 0.0 us)
Async XLA Ops:
  250.2 3.1 %copy-start = (f32[16,16,128]{2,1,0:T(8,128)}, f32[16,16,128]{2,1,0:T(8,128)S(1)}, u32[]{:S(2)}) copy-start(f32[16,16,128]{2,1,0:T(8,128)S(1)} %slice_dynamic-update-slice_fusion) | copy-start | bytes 393220

commit v2 on v1

v2 whole, which is shorter than its diff:
```python
import jax
import jax.numpy as jnp
from jax import lax
from jax.experimental import pallas as pl
from jax.experimental.pallas import tpu as pltpu
from jax.sharding import PartitionSpec as P

MESH = pl.DeviceIdType.MESH
WIDTH = 512
ITERS = 3
PENALTY = 0.2
RING = 8
LAG = 7
COUNTS = (11, 11, 10)
CHUNK = 2
CHUNKS = 176
STEPS = CHUNKS + 8 * LAG
SLOTS = 2 * LAG
F32 = jnp.float32
BF16 = jnp.bfloat16
DEEP = 1024
PLUS, MINUS, ACROSS, OWN = 0, 1, 2, 3


def halves(x):
    high = x.astype(BF16)
    return high, (x - high.astype(F32)).astype(BF16)


def matmul(a, b, dims):
    return lax.dot_general(a, b, (dims, ((), ())), preferred_element_type=F32)


def kernel(order, steps, image, panel, sinogram, out, duals,
           recv, staging, turns, updates, u, w, acc, high, low, above, below, flux,
           fwd, shares, changes,
           recv_sem, send_sem, own_sem, halo_send, halo_recv, sum_send, sum_recv, all_send, all_recv):
    col, tile = lax.axis_index("col"), lax.axis_index("tile")
    tiles = lax.axis_size("tile")
    rail, z = col // RING, lax.rem(col, RING)
    up = rail * RING + lax.rem(z + 1, RING)
    down = rail * RING + lax.rem(z + RING - 1, RING)
    partner = (1 - rail) * RING + z
    next_tile, prev_tile = lax.rem(tile + 1, tiles), lax.rem(tile + tiles - 1, tiles)
    links = ((PLUS, up), (MINUS, down), (ACROSS, partner))

    blocks = panel.shape[3] // 128
    def own_copy(tree, block):
        count = COUNTS[tree]
        return pltpu.make_async_copy(
            panel.at[0, pl.ds(sum(COUNTS[:tree]), count), :,
                     pl.ds(pl.multiple_of(block * 128, 128), 128)],
            recv.at[OWN, tree, pl.ds(block * count, count)],
            own_sem.at[tree, block],
        )

    for tree in range(3):
        @pl.loop(0, blocks)
        def _(block, tree=tree):
            own_copy(tree, block).start()

    barrier = pltpu.get_barrier_semaphore()
    for _, where in links:
        pl.semaphore_signal(barrier, inc=1, device_id={"col": where}, device_id_type=MESH)
    for d in range(1, tiles):
        pl.semaphore_signal(
            barrier, inc=1, device_id={"tile": lax.rem(tile + d, tiles)}, device_id_type=MESH)
    pl.semaphore_wait(barrier, tiles + 2)

    def halo_copies(source, m):
        last = source.shape[0] - WIDTH
        return (
            pltpu.make_async_remote_copy(
                source.at[pl.ds(0, WIDTH)], below.at[m], halo_send.at[m, 0], halo_recv.at[m, 0],
                device_id={"tile": prev_tile}, device_id_type=MESH),
            pltpu.make_async_remote_copy(
                source.at[pl.ds(last, WIDTH)], above.at[m], halo_send.at[m, 1], halo_recv.at[m, 1],
                device_id={"tile": next_tile}, device_id_type=MESH),
        )

    for copy in halo_copies(image, 0):
        copy.start()

    early = 2
    for tree in range(3):
        for block in range(early):
            own_copy(tree, block).wait()

    plans = []
    for k in range(ITERS):
        i = lax.rem(z - lax.rem(order[k], RING) + RING, RING)
        same = lax.div(order[k], RING) == rail
        root = same & (i == 0)
        flags = (root, ~same & ((i == 0) | (i == 4)), ~same & ((i == 0) | (i == 5)), i <= 4)
        for n, flag in enumerate(flags):
            turns[k, n] = jnp.full((8, 128), flag.astype(jnp.int32))
        link = (
            jnp.where(same | (i == 0) | (i > 4), PLUS, ACROSS),
            jnp.where(same | (i <= 4), MINUS, ACROSS),
            jnp.where(same | (i == 0), ACROSS, jnp.where(i <= 4, PLUS, MINUS)),
        )
        depth = (
            jnp.where(same, i, jnp.where(i == 0, 9, i + 1)),
            jnp.where(same, 8 - i, 9 - i),
            jnp.where(same, jnp.where(i <= 4, i + 2, 10 - i), jnp.where(i <= 4, i + 1, 9 - i)),
        )
        plans.append([
            (jnp.where(root, OWN, link[tree]), jnp.where(root, tree, k),
             jnp.where(root, 0, (depth[tree] - 1) * (LAG * CHUNK)))
            for tree in range(3)])

    def hop(link, where, step, slot):
        return pltpu.make_async_remote_copy(
            staging.at[slot, link],
            recv.at[link, :, pl.ds(step * CHUNK, CHUNK)],
            send_sem.at[slot, link], recv_sem.at[slot, link],
            device_id={"col": where}, device_id_type=MESH)

    def arrival(link, step, slot):
        ref = recv.at[link, :, pl.ds(step * CHUNK, CHUNK)]
        return pltpu.make_async_copy(ref, ref, recv_sem.at[slot, link])

    def chunk(link, k, step):
        return recv[link, k, pl.ds(step * CHUNK, CHUNK)]

    for step in range(LAG):
        for tree, (link, where) in enumerate(links):
            for k in range(ITERS):
                staging[step, link, k] = chunk(OWN, tree, step)
        for link, where in links:
            hop(link, where, step, step).start()

    for tree in range(3):
        @pl.loop(early, blocks)
        def _(block, tree=tree):
            own_copy(tree, block).wait()

    def relay(step):
        slot = lax.rem(step, SLOTS)
        came = step - LAG
        for link, _ in links:
            arrival(link, came, lax.rem(came, SLOTS)).wait()

        @pl.when(step >= SLOTS)
        def _():
            for link, where in links:
                hop(link, where, step - SLOTS, slot).wait_send()

        mine = jnp.minimum(step, CHUNKS - 1)
        for k in range(ITERS):
            plus, minus, across = (chunk(link, k, came) for link in (PLUS, MINUS, ACROSS))
            root, first_turn, second_turn, near = (
                jnp.broadcast_to(turns[k, n] == 1, (CHUNK, 8, 128)) for n in range(4))
            staging[slot, PLUS, k] = jnp.where(
                root, chunk(OWN, 0, mine), jnp.where(first_turn, across, plus))
            staging[slot, MINUS, k] = jnp.where(
                root, chunk(OWN, 1, mine), jnp.where(second_turn, across, minus))
            staging[slot, ACROSS, k] = jnp.where(
                root, chunk(OWN, 2, mine), jnp.where(near, plus, minus))
        for link, where in links:
            hop(link, where, step, slot).start()

    dual_step, primal_step, extrapolate = steps[0], steps[1], steps[2]
    rows_local = u.shape[1] // WIDTH
    column = lax.broadcasted_iota(jnp.int32, (WIDTH, 128), 0)
    inner = column < WIDTH - 1
    top = jnp.full((WIDTH, 128), tile) == 0
    bottom = jnp.full((WIDTH, 128), tile) == tiles - 1

    def fluxes(row, under, cut):
        across = jnp.where(inner, pltpu.roll(row, WIDTH - 1, 0) - row, 0.0)
        drop = under - row
        if cut is not None:
            drop = jnp.where(cut, 0.0, drop)
        inverse = 1.0 / jnp.sqrt(across * across + drop * drop + 1.0)
        return across * inverse, drop * inverse

    def smooth_begin(source, m):
        for copy in halo_copies(source, m):
            copy.wait()
        flux[...] = jnp.where(top, 0.0, fluxes(above[m], source[pl.ds(0, WIDTH), :], None)[1])

    def smooth_row(source, target, start, under, cut):
        row = source[pl.ds(start, WIDTH), :]
        right, drop = fluxes(row, under, cut)
        div = right - pltpu.roll(right, 1, 0) + drop - flux[...]
        flux[...] = drop
        target[pl.ds(start, WIDTH), :] = row + primal_step * PENALTY * div

    def smooth(source, m, target, beside=lambda r: None):
        smooth_begin(source, m)

        @pl.loop(0, rows_local - 1)
        def _(r):
            start = pl.multiple_of(r * WIDTH, WIDTH)
            under = source[pl.ds(pl.multiple_of(start + WIDTH, WIDTH), WIDTH), :]
            smooth_row(source, target, start, under, None)
            beside(r)

        smooth_row(source, target, (rows_local - 1) * WIDTH, below[m], bottom)

    def row_at(source, r):
        return source[pl.ds(pl.multiple_of(r * WIDTH, WIDTH), WIDTH), :]

    def smooth_inner(source, target):
        flux[...] = fluxes(row_at(source, 0), row_at(source, 1), None)[1]

        @pl.loop(1, rows_local - 1)
        def _(r):
            smooth_row(source, target, pl.multiple_of(r * WIDTH, WIDTH), row_at(source, r + 1), None)

    def smooth_edges(source, m, target):
        for copy in halo_copies(source, m):
            copy.wait()
        smooth_row(source, target, (rows_local - 1) * WIDTH, below[m], bottom)
        flux[...] = jnp.where(top, 0.0, fluxes(above[m], row_at(source, 0), None)[1])
        smooth_row(source, target, 0, row_at(source, 1), None)

    settled = LAG + 24
    pl.loop(LAG, settled)(relay)
    smooth(image, 0, u.at[0], lambda r: relay(settled + r))
    pl.loop(settled + rows_local - 1, STEPS)(relay)
    for step in range(STEPS - LAG, STEPS):
        for link, _ in links:
            arrival(link, step, step % SLOTS).wait()
    for step in range(STEPS - SLOTS, STEPS):
        for link, where in links:
            hop(link, where, step, step % SLOTS).wait_send()

    pairs = blocks // 2

    def gather(k, begin, end):
        plan = plans[k]

        @pl.loop(begin, end)
        def _(q):
            def part(b):
                return jnp.concatenate([
                    recv[plan[tree][0], plan[tree][1], plan[tree][2] + (b * COUNTS[tree] + n)]
                    for tree in range(3) for n in range(COUNTS[tree])], axis=0)

            at = pl.ds(pl.multiple_of(q * 256, 256), 256)
            p_high, p_low = halves(jnp.concatenate([part(2 * q), part(2 * q + 1)], axis=1))
            high[k % 2, :, at] = p_high
            low[k % 2, :, at] = p_low

    gather(0, 0, pairs)
    for k in range(ITERS):
        now = u.at[k]
        fwd[k] = jnp.zeros((256, 128), F32)

        @pl.loop(0, blocks * 128 // DEEP)
        def _(q, now=now, k=k):
            at = pl.ds(pl.multiple_of(q * DEEP, DEEP), DEEP)
            x_high, x_low = halves(now[at, :])
            p_high = high[k % 2, :, at]
            both = matmul(p_high, jnp.concatenate([x_high, x_low], axis=1), ((1,), (0,)))
            rest = matmul(low[k % 2, :, at], x_high, ((1,), (0,)))
            fwd[k] += both[:, :128] + (both[:, 128:] + rest)

        def share(d, k=k):
            to = lax.rem(tile + d, tiles)
            return pltpu.make_async_remote_copy(
                fwd.at[k, pl.ds(pl.multiple_of(to * 16, 16), 16)], shares.at[k, d - 1],
                sum_send.at[k, d - 1], sum_recv.at[k, d - 1],
                device_id={"tile": to}, device_id_type=MESH)

        for d in range(1, tiles):
            share(d).start()
        for copy in halo_copies(now, k + 1):
            copy.start()

        if k < ITERS - 1:
            gather(k + 1, 0, pairs)

        mine = pl.ds(pl.multiple_of(tile * 16, 16), 16)
        total = fwd[k, mine, :]
        for d in range(1, tiles):
            share(d).wait()
            total = total + shares[k, d - 1]
        current = jnp.zeros((16, 128), F32)
        for j in range(k):
            again = jnp.full((16, 128), (order[j] == order[k]).astype(jnp.int32)) == 1
            current = jnp.where(again, updates[j], current)
        measured = sinogram[order[k]]
        updated = (current + dual_step * total - dual_step * measured) / (1.0 + dual_step)
        updates[k] = updated
        changes[k, mine, :] = updated - current

        def spread(d, k=k, mine=mine):
            return pltpu.make_async_remote_copy(
                changes.at[k, mine], changes.at[k, mine],
                all_send.at[k, d - 1], all_recv.at[k, d - 1],
                device_id={"tile": lax.rem(tile + d, tiles)}, device_id_type=MESH)

        def spread_to_me(d, k=k):
            rows = changes.at[k, pl.ds(
                pl.multiple_of(lax.rem(tile + tiles - d, tiles) * 16, 16), 16)]
            return pltpu.make_async_copy(rows, rows, all_recv.at[k, d - 1])

        for d in range(1, tiles):
            spread(d).start()
        smooth_inner(now, w)
        for d in range(1, tiles):
            spread(d).wait_send()
            spread_to_me(d).wait()
        c_high, c_low = halves(changes[k])
        c_both = jnp.concatenate([c_high, c_low], axis=1)

        def push(q, k=k, c_high=c_high, c_both=c_both):
            at = pl.ds(pl.multiple_of(q * WIDTH, WIDTH), WIDTH)
            both = matmul(high[k % 2, :, at], c_both, ((0,), (0,)))
            rest = matmul(low[k % 2, :, at], c_high, ((0,), (0,)))
            adjoint = both[:, :128] + (both[:, 128:] + rest)
            gathered = adjoint if k == 0 else acc[at, :] + adjoint
            if k < ITERS - 1:
                acc[at, :] = gathered
            pushed = gathered + extrapolate * 16.0 * adjoint
            result = w[at, :] - primal_step * pushed
            if k < ITERS - 1:
                u[k + 1, at, :] = result
            else:
                out[at, :] = result

        pl.loop(1, rows_local - 1)(push)
        smooth_edges(now, k + 1, w)
        pl.loop(0, rows_local, step=rows_local - 1)(push)

    for subset in range(duals.shape[0]):
        final = jnp.zeros((16, 128), F32)
        for k in range(ITERS):
            here = jnp.full((16, 128), (order[k] == subset).astype(jnp.int32)) == 1
            final = jnp.where(here, updates[k], final)
        duals[subset] = final


def per_device(initial_image, panels, sinogram, subset_order, step_sizes):
    pixels, channels = initial_image.shape
    rays = sinogram.shape[1]
    tiles = lax.axis_size("tile")
    tiled = panels.reshape(panels.shape[0], panels.shape[1] // 8, 8, panels.shape[2])
    vmem = pl.BlockSpec(memory_space=pltpu.VMEM)
    smem = pl.BlockSpec(memory_space=pltpu.SMEM)
    dma = pltpu.SemaphoreType.DMA
    blocks = panels.shape[2] // 128
    return pl.pallas_call(
        kernel,
        out_shape=(jax.ShapeDtypeStruct((pixels, channels), F32),
                   jax.ShapeDtypeStruct(sinogram.shape, F32)),
        in_specs=[smem, smem, vmem, pl.BlockSpec(memory_space=pl.ANY), vmem],
        out_specs=(vmem, vmem),
        scratch_shapes=[
            pltpu.VMEM((4, ITERS, STEPS * CHUNK, 8, 128), F32),
            pltpu.VMEM((SLOTS, 3, ITERS, CHUNK, 8, 128), F32),
            pltpu.VMEM((ITERS, 4, 8, 128), jnp.int32),
            pltpu.VMEM((ITERS, rays, channels), F32),
            pltpu.VMEM((ITERS, pixels, channels), F32),
            pltpu.VMEM((pixels, channels), F32),
            pltpu.VMEM((pixels, channels), F32),
            pltpu.VMEM((2, rays * tiles, blocks * 128), BF16),
            pltpu.VMEM((2, rays * tiles, blocks * 128), BF16),
            pltpu.VMEM((ITERS + 1, WIDTH, channels), F32),
            pltpu.VMEM((ITERS + 1, WIDTH, channels), F32),
            pltpu.VMEM((WIDTH, channels), F32),
            pltpu.VMEM((ITERS, rays * tiles, channels), F32),
            pltpu.VMEM((ITERS, tiles - 1, rays, channels), F32),
            pltpu.VMEM((ITERS, rays * tiles, channels), F32),
            dma((SLOTS, 3)), dma((SLOTS, 3)), dma((3, blocks)),
            dma((ITERS + 1, 2)), dma((ITERS + 1, 2)),
            dma((ITERS, tiles - 1)), dma((ITERS, tiles - 1)),
            dma((ITERS, tiles - 1)), dma((ITERS, tiles - 1)),
        ],
        compiler_params=pltpu.CompilerParams(
            collective_id=0, has_side_effects=True, vmem_limit_bytes=62 * 1024 * 1024),
    )(subset_order, step_sizes, initial_image, tiled, sinogram)


def solution(mesh):
    in_specs = (P("tile", "col"), P("col", None, "tile"), P(None, "tile", "col"), P(), P())
    out_specs = (P("tile", "col"), P(None, "tile", "col"))
    return jax.shard_map(
        per_device, mesh=mesh, in_specs=in_specs, out_specs=out_specs, check_vma=False
    )
```

time: 254 us -> 205 us (0.81)
  Pallas kernels: 235 us -> 201 us
  local copies, waits for them, and re-layouts: 9.45 us -> 3.74 us
  between operations: 6.25 us -> 0.65 us
  other arithmetic: 2.86 us -> 0 us
    pallas_call x1, Pallas kernels: 235 us -> 201 us  [per_device(): pl.pallas_call(kernel, out_shape=(jax.ShapeDtypeStruct((pixels, channels)...]
where the time goes in v2:
time: 205 us
  Pallas kernels  201 us (98%)
  local copies, waits for them, and re-layouts  3.74 us (2%)
    pallas_call x1, Pallas kernels, per_device(): pl.pallas_call(kernel, out_shape=(jax.ShapeDtypeStruct((pixels, channels)...  201 us

profile of v2, /device:TPU:1, one launch (start us, length us, event | category | flops | bytes accessed | tf_op | source)
XLA Modules:
  0.0 205.2 jit_solution(8792696647309016582)
XLA Ops:
  0.6 200.8 %shard_map.68 = (f32[4096,128]{1,0:T(8,128)}, f32[16,16,128]{2,1,0:T(8,128)}) custom-call(s32[3]{0:T(128)} %order.1, f32[3]{0:T(128)} %steps.1, f32[4096,128]{1,0:T(8,128)} %image.1, f32[1,32,8,4096]{3,2,1,0:T(8,128)} %bitcast.1, f32[16,16,128]{2,1,0:T(8,128)} %sinogram.1), custom_call_target="tpu_custom_call" | custom-call | tf_op jit(solution)/shard_map/pallas_call | solution.py:346
  201.5 0.0 copy-start
  201.5 3.1 %copy.9 = f32[4096,128]{1,0:T(8,128)} copy(f32[4096,128]{1,0:T(8,128)} %get-tuple-element.4) | data formatting | bytes 4194304
  204.6 0.0 copy-done
  204.6 0.7 copy.10
Async XLA Ops:
  201.5 3.1 %copy-start = (f32[16,16,128]{2,1,0:T(8,128)S(1)}, f32[16,16,128]{2,1,0:T(8,128)}, u32[]{:S(2)}) copy-start(f32[16,16,128]{2,1,0:T(8,128)} %get-tuple-element.5) | copy-start | bytes 393220

commit v3 on v2

--- a/solution.py
+++ b/solution.py
@@ -67,16 +67,15 @@
             barrier, inc=1, device_id={"tile": lax.rem(tile + d, tiles)}, device_id_type=MESH)
     pl.semaphore_wait(barrier, tiles + 2)
 
+    def halo_copy(source, m, side):
+        where, row, to = (
+            (prev_tile, 0, below), (next_tile, source.shape[0] - WIDTH, above))[side]
+        return pltpu.make_async_remote_copy(
+            source.at[pl.ds(row, WIDTH)], to.at[m], halo_send.at[m, side], halo_recv.at[m, side],
+            device_id={"tile": where}, device_id_type=MESH)
+
     def halo_copies(source, m):
-        last = source.shape[0] - WIDTH
-        return (
-            pltpu.make_async_remote_copy(
-                source.at[pl.ds(0, WIDTH)], below.at[m], halo_send.at[m, 0], halo_recv.at[m, 0],
-                device_id={"tile": prev_tile}, device_id_type=MESH),
-            pltpu.make_async_remote_copy(
-                source.at[pl.ds(last, WIDTH)], above.at[m], halo_send.at[m, 1], halo_recv.at[m, 1],
-                device_id={"tile": next_tile}, device_id_type=MESH),
-        )
+        return halo_copy(source, m, 0), halo_copy(source, m, 1)
 
     for copy in halo_copies(image, 0):
         copy.start()
@@ -172,7 +171,7 @@
         drop = under - row
         if cut is not None:
             drop = jnp.where(cut, 0.0, drop)
-        inverse = 1.0 / jnp.sqrt(across * across + drop * drop + 1.0)
+        inverse = lax.rsqrt(across * across + drop * drop + 1.0)
         return across * inverse, drop * inverse
 
     def smooth_begin(source, m):
@@ -216,7 +215,7 @@
         flux[...] = jnp.where(top, 0.0, fluxes(above[m], row_at(source, 0), None)[1])
         smooth_row(source, target, 0, row_at(source, 1), None)
 
-    settled = LAG + 24
+    settled = LAG + 96
     pl.loop(LAG, settled)(relay)
     smooth(image, 0, u.at[0], lambda r: relay(settled + r))
     pl.loop(settled + rows_local - 1, STEPS)(relay)
@@ -267,8 +266,7 @@
 
         for d in range(1, tiles):
             share(d).start()
-        for copy in halo_copies(now, k + 1):
-            copy.start()
+        halo_copy(now, k + 1, 1).start()
 
         if k < ITERS - 1:
             gather(k + 1, 0, pairs)
@@ -300,6 +298,7 @@
 
         for d in range(1, tiles):
             spread(d).start()
+        halo_copy(now, k + 1, 0).start()
         smooth_inner(now, w)
         for d in range(1, tiles):
             spread(d).wait_send()
@@ -371,7 +370,7 @@
             dma((ITERS, tiles - 1)), dma((ITERS, tiles - 1)),
         ],
         compiler_params=pltpu.CompilerParams(
-            collective_id=0, has_side_effects=True, vmem_limit_bytes=62 * 1024 * 1024),
+            collective_id=0, has_side_effects=True, vmem_limit_bytes=51 * 1024 * 1024),
     )(subset_order, step_sizes, initial_image, tiled, sinogram)
 
 

time: 205 us -> 200 us (0.976)
  Pallas kernels: 201 us -> 195 us
    pallas_call x1, Pallas kernels: 201 us -> 195 us  [per_device(): pl.pallas_call(kernel, out_shape=(jax.ShapeDtypeStruct((pixels, channels)...]
    unnamed x4 -> x8, local copies, waits for them, and re-layouts: 3.74 us -> 4.18 us
where the time goes in v3:
time: 200 us; the launch traced here: 199 us
  Pallas kernels  195 us (98%)
  local copies, waits for them, and re-layouts  4.18 us (2%)
    pallas_call x1, Pallas kernels, per_device(): pl.pallas_call(kernel, out_shape=(jax.ShapeDtypeStruct((pixels, channels)...  195 us
    unnamed x8, local copies, waits for them, and re-layouts  4.18 us

profile of v3, /device:TPU:1, one launch (start us, length us, event | category | flops | bytes accessed | tf_op | source)
XLA Modules:
  0.0 199.5 jit_solution(15872403782224333250)
XLA Ops:
  0.6 0.0 copy-start
  0.6 0.9 copy-done
  1.5 0.0 copy-start.1
  1.5 0.7 copy-done.1
  2.2 0.0 copy-start.2
  2.2 0.7 copy-done.2
  2.8 194.7 %shard_map.68 = (f32[4096,128]{1,0:T(8,128)S(1)}, f32[16,16,128]{2,1,0:T(8,128)S(1)}) custom-call(s32[3]{0:T(128)S(1)} %copy-done.1, f32[3]{0:T(128)S(1)} %copy-done.2, f32[4096,128]{1,0:T(8,128)} %image.1, f32[1,32,8,4096]{3,2,1,0:T(8,128)} %bitcast.1, f32[16,16,128]{2,1,0:T(8,128)S(1)} %copy-done), custom_call_target="tpu_custom_call" | custom-call | tf_op jit(solution)/shard_map/pallas_call | solution.py:345
  197.5 1.3 copy.9
  198.8 0.7 copy.10
Async XLA Ops:
  0.6 0.9 copy-start
  1.5 0.7 copy-start.1
  2.2 0.7 copy-start.2
